TPU v7x, 32 devices: a whole 2x2x4 slice. The times are simulated.
32 devices in a mesh: cuts: 4 (over z), dev: 8 (over y, x, core).
Axes of the slice: x: 2, y: 2, z: 4, core: 2. Of those that a mesh axis runs over, the one named last changes fastest.
Arguments:
- inputs: bfloat16 [16384, 3072], P(('cuts', 'dev')), may hold values from -6 to 6
- cotangent: bfloat16 [16384, 512], P(('cuts', 'dev')), may hold values from -0.29882812 to 0.29882812
- errors: bfloat16 [32, 3072, 512], P(('cuts', 'dev')), may hold values from -6 to 6
- previous_q: float32 [512, 64], replicated, may hold values from -0.25 to 0.25
Outputs:
- new_errors: bfloat16 [32, 3072, 512], P(('cuts', 'dev'))
- p_hat: float32 [3072, 64], replicated
- q_mean: float32 [512, 64], replicated
All inputs are finite; a program needn't handle non-finite values.
Results may differ from a plain program's by a relative error of at most 0.001.
Values sent between devices are 32-bit elements; how exact they have to be, the bound alone decides.
No kernel may reach another device: no remote copies, remote signals or barrier semaphores. Data moves between devices by JAX's collectives and lax.ppermute only.
A program may use at most 64 MiB of HBM per device.

v0:
```python
import jax
import jax.numpy as jnp
from jax import lax
from jax.sharding import PartitionSpec as P

HI = lax.Precision.HIGHEST


def solve_factor(gram, p_rows):
    lower = jnp.linalg.cholesky(gram)
    return lax.linalg.triangular_solve(lower, p_rows, left_side=False, lower=True, transpose_a=True)


def contract_rows(left, right):
    return lax.dot_general(
        left, right, (((0,), (0,)), ((), ())), precision=HI, preferred_element_type=jnp.float32
    )


def body(inputs, cotangent, errors, previous_q):
    grad = lax.dot_general(
        inputs, cotangent, (((0,), (0,)), ((), ())), preferred_element_type=jnp.float32
    )
    merged = grad + errors[0].astype(jnp.float32)
    devices = lax.axis_size("cuts") * lax.axis_size("dev")
    p_share = lax.psum_scatter(
        jnp.dot(merged, previous_q, precision=HI), "dev", scatter_dimension=0, tiled=True
    )
    p_share = lax.psum(p_share, "cuts")
    gram = lax.psum(contract_rows(p_share, p_share), "dev")
    hat_share = solve_factor(gram, p_share)
    p_hat = lax.all_gather(hat_share, "dev", axis=0, tiled=True)
    q_share = lax.psum_scatter(contract_rows(merged, p_hat), "dev", scatter_dimension=0, tiled=True)
    q_share = lax.psum(q_share, "cuts")
    q_sum = lax.all_gather(q_share, "dev", axis=0, tiled=True)
    q_mean = q_sum / devices
    approx = jnp.dot(p_hat, q_mean.T, precision=HI)
    new_errors = (merged - approx).astype(jnp.bfloat16)[None]
    return (new_errors, p_hat, q_mean)


def solution(mesh):
    in_specs = (
        P(("cuts", "dev"), None),
        P(("cuts", "dev"), None),
        P(("cuts", "dev"), None, None),
        P(),
    )
    out_specs = (P(("cuts", "dev"), None, None), P(), P())
    return jax.shard_map(body, mesh=mesh, in_specs=in_specs, out_specs=out_specs, check_vma=False)
```

profile of v0, /device:TPU:0, one launch (start us, length us, event | category | flops | bytes accessed | tf_op | source)
XLA Modules:
  0.0 238.6 jit_solution(2747192408776111508)
XLA Ops:
  7.2 0.0 copy-start
  7.2 0.0 copy-start.3
  7.2 0.0 reduce-scatter.3.cloned.1.call-start
  7.2 1.8 copy-done
  9.1 4.0 %convert_add_fusion = f32[3072,512]{1,0:T(8,128)S(1)} fusion(bf16[512,3072]{1,0:T(8,128)(2,1)S(1)} %copy-done, bf16[512,512]{1,0:T(8,128)(2,1)} %param.5, bf16[1,3072,512]{2,1,0:T(8,128)(2,1)} %param.6), kind=kOutput, calls=%fused_computation | convolution fusion | flops 1613758464 | bytes 13107200 | tf_op jit(solution)/shard_map/dot_general | solution.py:21
  13.0 0.0 copy-start.1
  13.1 2.7 %copy-done.1 = f32[3072,512]{1,0:T(8,128)} copy-done((f32[3072,512]{1,0:T(8,128)}, f32[3072,512]{1,0:T(8,128)S(1)}, u32[]{:S(2)}) %copy-start.1) | copy-done | bytes 6291480
  15.7 7.1 %fusion.5 = f32[3072,64]{0,1:T(8,128)} fusion(f32[3072,512]{1,0:T(8,128)S(1)} %convert_add_fusion, f32[512,64]{0,1:T(8,128)S(1)} %copy-done.3), kind=kOutput, calls=%fused_computation.14 | convolution fusion | flops 1207959552 | bytes 7208960 | tf_op jit(solution)/shard_map/dot_general | solution.py:27
  22.8 0.0 reduce-scatter.3.cloned.1.call-update
  22.8 0.0 all-reduce.2.cloned.1.call-start
  22.9 37.8 %reduce-scatter.3.cloned.1.call-done = f32[384,64]{0,1:T(8,128)} async-done(((f32[3072,64]{0,1:T(8,128)}), f32[384,64]{0,1:T(8,128)}) %reduce-scatter.3.cloned.1.call-update) | async-done | bytes 98320 | tf_op jit(solution)/shard_map/reduce_scatter | solution.py:26
  60.6 0.0 all-reduce.2.cloned.1.call-update
  60.7 0.0 reduce-scatter.5.cloned.1.call-start
  60.7 36.7 %all-reduce.2.cloned.1.call-done = f32[384,64]{0,1:T(8,128)} async-done(((f32[384,64]{0,1:T(8,128)}), f32[384,64]{0,1:T(8,128)}) %all-reduce.2.cloned.1.call-update) | async-done | bytes 98320 | tf_op jit(solution)/shard_map/psum | solution.py:29
  97.4 1.2 fusion.6
  98.7 22.4 %psum.22 = f32[64,64]{0,1:T(8,128)S(1)} all-reduce(f32[64,64]{0,1:T(8,128)S(1)} %fusion.6), channel_id=1, replica_groups=mesh['cuts'=4,'dev'=8] {'dev'}, use_global_device_ids=true, to_apply=%region_2.0 | all-reduce | flops 4096 | bytes 32768 | tf_op jit(solution)/shard_map/psum | solution.py:30
  121.0 0.1 copy.8
  121.1 5.8 %cholesky.16 = f32[64,64]{1,0:T(8,128)S(1)} custom-call(f32[64,64]{1,0:T(8,128)S(1)} %fusion.4), custom_call_target="Cholesky" | custom-call | tf_op jit(solution)/shard_map/jit(cholesky)/cholesky | solution.py:10
  127.0 0.6 compare_reduce_fusion
  127.6 0.7 fusion.1
  128.3 4.9 %custom-call.6 = f32[1,64,64]{1,2,0:T(8,128)S(1)} custom-call(f32[1,64,64]{2,1,0:T(8,128)S(1)} %fusion.1), custom_call_target="InvertDiagBlocksLowerTriangular" | custom-call | tf_op jit(solution)/shard_map/triangular_solve | solution.py:11
  133.2 1.2 fusion.2
  134.4 11.1 %all_gather.6 = f32[3072,64]{0,1:T(8,128)S(1)} all-gather(f32[384,64]{0,1:T(8,128)S(1)} %fusion.2), channel_id=1, replica_groups=mesh['cuts'=4,'dev'=8] {'dev'}, dimensions={0}, use_global_device_ids=true | all-gather | bytes 884736 | tf_op jit(solution)/shard_map/all_gather | solution.py:32
  145.5 0.9 copy-done.2
  146.4 12.7 %fusion.7 = f32[512,64]{1,0:T(8,128)} fusion(f32[3072,512]{1,0:T(8,128)} %copy-done.1, f32[3072,64]{0,1:T(8,128)S(1)} %all_gather.6), kind=kOutput, calls=%fused_computation.16 | convolution fusion | flops 1207959552 | bytes 7208960 | tf_op jit(solution)/shard_map/dot_general | solution.py:15
  159.1 0.0 reduce-scatter.5.cloned.1.call-update
  159.1 32.7 %reduce-scatter.5.cloned.1.call-done = f32[64,64]{1,0:T(8,128)} async-done(((f32[512,64]{1,0:T(8,128)}), f32[64,64]{1,0:T(8,128)}) %reduce-scatter.5.cloned.1.call-update) | async-done | bytes 16400 | tf_op jit(solution)/shard_map/reduce_scatter | solution.py:33
  191.8 19.6 %psum.23 = f32[64,64]{1,0:T(8,128)S(1)} all-reduce(f32[64,64]{1,0:T(8,128)} %reduce-scatter.5.cloned.1.call-done), channel_id=1, replica_groups=mesh['cuts'=4,'dev'=8] {'cuts'}, use_global_device_ids=true, to_apply=%region_6.7 | all-reduce | flops 4096 | bytes 32768 | tf_op jit(solution)/shard_map/psum | solution.py:34
  211.4 9.2 %all_gather.7 = f32[512,64]{1,0:T(8,128)S(1)} all-gather(f32[64,64]{1,0:T(8,128)S(1)} %psum.23), channel_id=1, replica_groups=mesh['cuts'=4,'dev'=8] {'dev'}, dimensions={0}, use_global_device_ids=true | all-gather | bytes 147456 | tf_op jit(solution)/shard_map/all_gather | solution.py:35
  220.6 8.6 %fusion = bf16[1,3072,512]{2,1,0:T(8,128)(2,1)} fusion(f32[3072,512]{1,0:T(8,128)} %copy-done.1, f32[3072,64]{0,1:T(8,128)} %copy-done.2, f32[512,64]{1,0:T(8,128)S(1)} %all_gather.7), kind=kOutput, calls=%fused_computation.2 | convolution fusion | flops 1211138048 | bytes 10354688 | tf_op jit(solution)/shard_map/dot_general | solution.py:37
  229.2 0.8 copy.9
  230.0 2.1 copy.13
  (5 shorter events, 0.1 us)
Async XLA Ops:
  7.2 1.9 copy-start
  7.2 8.5 %copy-start.3 = (f32[512,64]{0,1:T(8,128)S(1)}, f32[512,64]{0,1:T(8,128)}, u32[]{:S(2)}) copy-start(f32[512,64]{0,1:T(8,128)} %param.7) | copy-start | bytes 393220
  7.2 53.5 %reduce-scatter.3.cloned.1.call-start = ((), (), s32[]{:S(2)}) async-start(), calls=%async_computation.2 | async-start | bytes 884736 | tf_op jit(solution)/shard_map/reduce_scatter | solution.py:26
  13.0 2.7 %copy-start.1 = (f32[3072,512]{1,0:T(8,128)}, f32[3072,512]{1,0:T(8,128)S(1)}, u32[]{:S(2)}) copy-start(f32[3072,512]{1,0:T(8,128)S(1)} %convert_add_fusion) | copy-start | bytes 18874372
  22.8 74.6 %all-reduce.2.cloned.1.call-start = ((), (), s32[]{:S(2)}) async-start(), calls=%async_computation.3 | async-start | bytes 196608 | tf_op jit(solution)/shard_map/psum | solution.py:29
  60.7 131.1 %reduce-scatter.5.cloned.1.call-start = ((), (), s32[]{:S(2)}) async-start(), calls=%async_computation.4 | async-start | bytes 294912 | tf_op jit(solution)/shard_map/reduce_scatter | solution.py:33
  145.5 0.9 copy-start.2
Sparse Core Ops, SparseCore 0:
  22.9 37.6 reduce-scatter.2
  63.0 34.4 all-reduce.1
  159.2 32.5 reduce-scatter.4
where the time goes:
time: 239 us
  waiting for transfers between devices  107 us (45%)
  blocking collectives  62.3 us (26%)
  matrix products  34.7 us (15%)
  between operations  13.8 us (6%)
  other arithmetic  12.1 us (5%)
  local copies, waits for them, and re-layouts  8.29 us (3%)
    reduce_scatter x1, waiting for transfers between devices, body(): lax.psum_scatter(jnp.dot(merged, previous_q, precision=HI), 'dev', scatte...  37.8 us
    psum x1, waiting for transfers between devices, body(): p_share = lax.psum(p_share, 'cuts')  36.7 us
    reduce_scatter x1, waiting for transfers between devices, body(): lax.psum_scatter(contract_rows(merged, p_hat), 'dev', scatter_dimension=0...  32.7 us
    psum x1, blocking collectives, body(): gram = lax.psum(contract_rows(p_share, p_share), 'dev')  22.4 us
    psum x1, blocking collectives, body(): q_share = lax.psum(q_share, 'cuts')  19.6 us
    dot_general x2, matrix products, contract_rows(): lax.dot_general(left, right, (((0,), (0,)), ((), ())), precision=HI, pref...  13.9 us
    all_gather x1, blocking collectives, body(): p_hat = lax.all_gather(hat_share, 'dev', axis=0, tiled=True)  11.1 us
    all_gather x1, blocking collectives, body(): q_sum = lax.all_gather(q_share, 'dev', axis=0, tiled=True)  9.24 us
  transfers between devices with their start and end apart: 3, of which 3 were waited for; matrix products, arithmetic and copies ran while one was open for 0% of the time, Pallas kernels for 0%

commit v1 on v0

v1 whole, which is shorter than its diff:
```python
import functools

import jax
import jax.numpy as jnp
from jax import lax
from jax.experimental import pallas as pl
from jax.experimental.pallas import tpu as pltpu
from jax.sharding import Mesh, PartitionSpec as P


F32 = jnp.float32
BF16 = jnp.bfloat16
LANES = 128
VM = pl.BlockSpec(memory_space=pltpu.VMEM)
HBM = pl.BlockSpec(memory_space=pltpu.HBM)
SM = pl.BlockSpec(memory_space=pltpu.SMEM)
NN = (((1,), (0,)), ((), ()))
NT = (((1,), (1,)), ((), ()))
TN = (((0,), (0,)), ((), ()))


def dot(a, b, dims, precision=None):
    return lax.dot_general(a, b, dims, precision=precision, preferred_element_type=F32)


def split3(x):
    high = x.astype(BF16)
    rest = x - high.astype(F32)
    mid = rest.astype(BF16)
    low = (rest - mid.astype(F32)).astype(BF16)
    return jnp.concatenate([high, mid, low], axis=0)


def fold3(x):
    rows = x.shape[0] // 3
    return x[:rows] + x[rows : 2 * rows] + x[2 * rows :]


def call(kernel, outs, ins_specs, out_specs, scratch, args, flops, limit=24):
    return pl.pallas_call(
        kernel,
        out_shape=outs,
        in_specs=ins_specs,
        out_specs=out_specs,
        scratch_shapes=scratch,
        compiler_params=pltpu.CompilerParams(vmem_limit_bytes=limit * 1024 * 1024),
        cost_estimate=pl.CostEstimate(flops=flops, bytes_accessed=0, transcendentals=0),
    )(*args)


def vmem(shape, dtype=F32):
    return jax.ShapeDtypeStruct(shape, dtype)


def left_half(total, block, start, xv, ev, v3, q3, ready=None):
    rank = v3.shape[0] // 3
    for i in range(total.shape[0] // rank * LANES // block):
        if ready is not None:
            ready(i)
        cut = pl.ds(pl.multiple_of(start + i * block, LANES), block)
        part = fold3(dot(v3[...], xv[:, cut], NN) + dot(q3[...], ev[cut, :], NT))
        for j in range(block // LANES):
            at = (i * (block // LANES) + j) * rank
            total[at : at + rank, :] = part[:, j * LANES : (j + 1) * LANES]


def put_chips(chips, ids, total, out):
    size = out.shape[0] // chips
    for chip in range(chips):
        start = pl.multiple_of((chip ^ ids[1]) * size, 8)
        out[chip * size : (chip + 1) * size, :] = total[pl.ds(start, size), :]


def first_kernel(cores, chips, block, ids, x_hbm, y_hbm, e_hbm, q_hbm, send, xv, yv, ev, v3, q3, q_ref, total, sem):
    depth = x_hbm.shape[1]
    half = depth // cores
    steps = half // block
    q_copy = pltpu.make_async_copy(q_hbm, q_ref, sem.at[0])
    y_copy = pltpu.make_async_copy(y_hbm, yv, sem.at[1])
    q_copy.start()
    y_copy.start()
    copies = []
    for k in range(cores):
        start = ((ids[0] + 1 + k) % cores) * half
        for i in range(steps):
            cut = pl.ds(pl.multiple_of(start + i * block, LANES), block)
            at = 2 + 2 * (k * steps + i)
            pair = (
                pltpu.make_async_copy(x_hbm.at[:, cut], xv.at[:, cut], sem.at[at]),
                pltpu.make_async_copy(e_hbm.at[0, cut, :], ev.at[cut, :], sem.at[at + 1]),
            )
            pair[0].start()
            pair[1].start()
            copies.append(pair)

    def ready(i):
        copies[i][0].wait()
        copies[i][1].wait()

    q_copy.wait()
    q3[...] = split3(q_ref[...])
    y_copy.wait()
    v3[...] = split3(fold3(dot(q3[...], yv[...], NT)))
    left_half(total, block, ((ids[0] + 1) % cores) * half, xv, ev, v3, q3, ready)
    put_chips(chips, ids, total, send)
    for i in range(steps, cores * steps):
        ready(i)


def second_kernel(chips, block, ids, xv, ev, v3, q3, keep, total):
    left_half(total, block, ids[0] * (total.shape[0] // (v3.shape[0] // 3) * LANES), xv, ev, v3, q3)
    put_chips(chips, ids, total, keep)


def sum_kernel(count, *refs):
    ins, outs = refs[:count], refs[count:]
    size = outs[0].shape[0]
    for k, out in enumerate(outs):
        rows = pl.ds(k * size, size)
        total = ins[0][rows, :]
        for other in ins[1:]:
            total = total + other[rows, :]
        out[...] = total


def add_up(ins, pieces):
    rows = ins[0].shape[0]
    shape = vmem((rows // pieces, LANES))
    return call(
        functools.partial(sum_kernel, len(ins)), [shape] * pieces, [VM] * len(ins), [VM] * pieces, [], ins, 10**7, 8
    )


def merge_kernel(span, xv, yv, ev, merged, parts):
    for i in range(ev.shape[0] // span):
        cut = slice(i * span, (i + 1) * span)
        block = dot(xv[:, cut], yv[...], TN) + ev[cut, :].astype(F32)
        merged[cut, :] = block
        high = block.astype(BF16)
        parts[2 * i * span : (2 * i + 1) * span, :] = high
        parts[(2 * i + 1) * span : (2 * i + 2) * span, :] = (block - high.astype(F32)).astype(BF16)


def chunk_of(chips, ids, where):
    return (where[0] ^ ids[0]) * chips + (where[1] ^ ids[1])


def chunk_kernel(chips, places, first, last, ids, *refs):
    parts, rest = refs[: len(places)], refs[len(places) :]
    merged2, rest = rest[0], rest[1:]
    before, rest = (None, rest) if first else (rest[0], rest[1:])
    p3 = rest[0]
    rank = p3.shape[0] // 3
    span = parts[0].shape[0] // rank * LANES
    t = None if first else before[...]
    for i, (part, where) in enumerate(zip(parts, places)):
        for c in range(span // LANES):
            at = i * span + c * LANES
            p3[:, at : at + LANES] = split3(part[c * rank : (c + 1) * rank, :])
        rows = pl.ds(pl.multiple_of(chunk_of(chips, ids, where) * (2 * span), 16), 2 * span)
        mine = p3[:, i * span : (i + 1) * span]
        new = dot(jnp.concatenate([mine, mine], axis=1), merged2[rows, :], NN)
        t = new if t is None else t + new
    if not last:
        rest[1][...] = t
        return
    keep, send, total = rest[1:]
    right = fold3(t)
    for c in range(right.shape[1] // LANES):
        total[c * rank : (c + 1) * rank, :] = right[:, c * LANES : (c + 1) * LANES]
    size = keep.shape[0]
    keep[...] = total[pl.ds(pl.multiple_of(ids[0] * size, 8), size), :]
    send[...] = total[pl.ds(pl.multiple_of((1 - ids[0]) * size, 8), size), :]


def gram_kernel(*refs):
    gram = refs[-1]
    rank = gram.shape[0]
    full = sum(dot(p3[...], p3[...], NT) for p3 in refs[:-1])
    full = fold3(full)
    gram[...] = full[:, :rank] + full[:, rank : 2 * rank] + full[:, 2 * rank :]


def factor_kernel(gram, lower_inv):
    rank = gram.shape[0]
    n = 8
    row = lax.broadcasted_iota(jnp.int32, (rank, rank), 0)
    lane = lax.broadcasted_iota(jnp.int32, (rank, rank), 1)
    eye = jnp.where(lane == row, 1.0, 0.0).astype(F32)
    work = jnp.concatenate([eye, gram[...]], axis=1)
    groups = [work[n * g : n * g + n, :] for g in range(rank // n)]
    wide = (n, 2 * rank)

    def column(x, k):
        return jnp.broadcast_to(x[:, rank + k : rank + k + 1], wide)

    def line(x, i):
        return jnp.broadcast_to(x[i : i + 1, :], wide)

    sub = lax.broadcasted_iota(jnp.int32, wide, 0)
    for g in range(rank // n):
        base = n * g
        cols = [column(groups[g], base + j) for j in range(n)]
        b = {(i, j): line(cols[j], i) for j in range(n) for i in range(j, n)}
        low, inv = {}, []
        for s in range(n):
            inv.append(1.0 / b[s, s])
            for i in range(s + 1, n):
                low[i, s] = b[i, s] * inv[s]
            for j in range(s + 1, n):
                for i in range(j, n):
                    b[i, j] = b[i, j] - low[i, s] * b[j, s]
        rows = []
        for i in range(n):
            r = line(groups[g], i)
            for s in range(i):
                r = r - low[i, s] * rows[s]
            rows.append(r)
        for h in range(g + 1, rank // n):
            x = [column(groups[h], base + s) for s in range(n)]
            for s in range(n):
                for t in range(s):
                    x[s] = x[s] - low[s, t] * x[t]
            new = groups[h]
            for s in range(n):
                new = new - (x[s] * inv[s]) * rows[s]
            groups[h] = new
        out = jnp.zeros(wide, F32)
        for i in range(n):
            out = jnp.where(sub == i, rows[i] * jnp.sqrt(inv[i]), out)
        lower_inv[base : base + n, :] = out[:, :rank]


def hat_kernel(cores, chips, places, ids, *refs):
    p3s, (lower_inv, p_hat, hat3) = refs[:-3], refs[-3:]
    rank = lower_inv.shape[0]
    inv3 = split3(lower_inv[...])
    at = 0
    for p3 in p3s:
        full = dot(inv3, p3[:rank, :], NN)
        mids = dot(inv3[: 2 * rank], p3[rank : 2 * rank, :], NN)
        hats = fold3(full) + (mids[:rank] + mids[rank:]) + dot(inv3[:rank], p3[2 * rank :, :], NN)
        span = p_hat.shape[1] // (cores * chips)
        for i in range(p3.shape[1] // span):
            start = chunk_of(chips, ids, places[at]) * span
            at += 1
            hat = hats[:, i * span : (i + 1) * span]
            p_hat[:, pl.ds(pl.multiple_of(start, LANES), span)] = hat
            for c in range(span // LANES):
                turned = hat[:, c * LANES : (c + 1) * LANES].T
                high = turned.astype(BF16)
                low = (turned - high.astype(F32)).astype(BF16)
                rows = pl.ds(pl.multiple_of(start + c * LANES, LANES), LANES)
                hat3[rows, :] = jnp.concatenate([high, low, high], axis=1)


def last_kernel(devices, block, ids, keep, other, lower_inv, hat, hat3, merged, new_errors, p_hat, q_mean, total, out, q_out, sem):
    copies = [pltpu.make_async_copy(hat, p_hat, sem.at[0])]
    copies[0].start()
    rank = lower_inv.shape[0]
    half = keep.shape[0]
    total[pl.ds(pl.multiple_of(ids[0] * half, 8), half), :] = keep[...]
    if other is not None:
        total[pl.ds(pl.multiple_of((1 - ids[0]) * half, 8), half), :] = other[...]
    wide = jnp.concatenate([total[c * rank : (c + 1) * rank, :] for c in range(total.shape[0] // rank)], axis=1)
    a, b = split3(lower_inv[...]), split3(wide)
    ah, am, al = a[:rank], a[rank : 2 * rank], a[2 * rank :]
    bh, bm, bl = b[:rank], b[rank : 2 * rank], b[2 * rank :]
    right = dot(jnp.concatenate([ah, ah, am, ah, al, am], axis=1), jnp.concatenate([bh, bm, bh, bl, bh, bm], axis=0), NN)
    right = right / devices
    high = right.astype(BF16)
    low = (right - high.astype(F32)).astype(BF16)
    q3 = jnp.concatenate([high, high, low], axis=0)
    q_out[...] = right
    copies.append(pltpu.make_async_copy(q_out, q_mean, sem.at[1]))
    copies[1].start()
    for i in range(merged.shape[0] // block):
        cut = pl.ds(i * block, block)
        out[cut, :] = (merged[cut, :] - dot(hat3[cut, :], q3, NN)).astype(BF16)
        copies.append(pltpu.make_async_copy(out.at[cut, :], new_errors.at[0, cut, :], sem.at[2 + i]))
        copies[2 + i].start()
    for copy in copies:
        copy.wait()


def exchange(parts, axis, size):
    return [parts[0]] + [swap(parts[k], axis, size, k) for k in range(1, size)]


def swap(x, axis, size, by):
    return lax.ppermute(x, axis, [(i, i ^ by) for i in range(size)])


def body(sizes, *args):
    return step(sizes, *args)


def step(sizes, inputs, cotangent, errors, previous_q):
    cores, chips, groups, cuts = sizes
    tokens, depth = inputs.shape
    width, rank = previous_q.shape
    devices = cores * chips * groups * cuts
    rows = depth * rank // LANES
    span = depth // (cores * chips)
    block = next(b for b in (512, 384, 256, LANES) if depth // cores % b == 0)
    steps = depth // block
    ids = jnp.stack([lax.axis_index("core"), lax.axis_index("chip")]).astype(jnp.int32)
    half = vmem((rows // cores, LANES))
    total = pltpu.VMEM((rows // cores, LANES), F32)
    send, xv, yv, ev, v3, q3 = call(
        functools.partial(first_kernel, cores, chips, block),
        [
            half,
            vmem((tokens, depth), BF16),
            vmem((tokens, width), BF16),
            vmem((depth, width), BF16),
            vmem((3 * rank, tokens), BF16),
            vmem((3 * rank, width), BF16),
        ],
        [SM] + [HBM] * 4,
        [VM] * 6,
        [pltpu.VMEM((rank, width), F32), total, pltpu.SemaphoreType.DMA((2 + 2 * steps,))],
        (ids, inputs, cotangent, errors, previous_q.T),
        10**9,
        46,
    )
    got = swap(send, "core", cores, 1)
    keep = call(
        functools.partial(second_kernel, chips, block),
        half,
        [SM] + [VM] * 4,
        VM,
        [total],
        (ids, xv, ev, v3, q3),
        10**9,
        8,
    )
    parts = add_up([keep, got], chips)
    parts = add_up(exchange(parts, "chip", chips), 1)
    if groups > 1:
        parts = add_up(exchange(parts * groups, "group", groups), 1)
    parts = add_up(exchange(parts * cuts, "cuts", cuts), 1)
    parts = exchange(parts * chips, "chip", chips)
    parts = parts + [swap(part, "core", cores, 1) for part in parts]

    merged, merged2 = call(
        functools.partial(merge_kernel, span),
        [vmem((depth, width)), vmem((2 * depth, width), BF16)],
        [VM] * 3,
        [VM] * 2,
        [],
        (xv, yv, ev),
        10**9,
        8,
    )
    places = [(core, chip) for core in range(cores) for chip in range(chips)]
    batches = [[0, chips], list(range(1, chips)), list(range(chips + 1, 2 * chips))]
    share = vmem((width * rank // LANES // cores, LANES))
    sums, p3s, order = [], [], []
    for at, batch in enumerate(batches):
        end = at == len(batches) - 1
        p3, *sums = call(
            functools.partial(chunk_kernel, chips, [places[k] for k in batch], at == 0, end),
            [vmem((3 * rank, span * len(batch)), BF16)] + ([share, share] if end else [vmem((3 * rank, width))]),
            [SM] + [VM] * (len(batch) + 1 + len(sums)),
            [VM] * (3 if end else 2),
            [pltpu.VMEM((width * rank // LANES, LANES), F32)] if end else [],
            (ids, *[parts[k] for k in batch], merged2, *sums),
            10**8,
            8,
        )
        p3s.append(p3)
        order += [places[k] for k in batch]
    keep, send = sums
    got = swap(send, "core", cores, 1)
    part = add_up([keep, got], 1)[0]
    part = add_up(exchange([part] * chips, "chip", chips), 1)[0]
    if groups > 1:
        part = add_up(exchange([part] * groups, "group", groups), 1)[0]
    part = add_up(exchange([part] * cuts, "cuts", cuts), 1)[0]
    other = swap(part, "core", cores, 1)

    gram = call(gram_kernel, vmem((rank, rank)), [VM] * len(p3s), VM, [], p3s, 10**8, 8)
    lower_inv = call(factor_kernel, vmem((rank, rank)), [VM], VM, [], (gram,), 10**9, 8)
    hat, hat3 = call(
        functools.partial(hat_kernel, cores, chips, order),
        [vmem((rank, depth)), vmem((depth, 3 * rank), BF16)],
        [SM] + [VM] * (len(p3s) + 1),
        [VM, VM],
        [],
        (ids, *p3s, lower_inv),
        10**9,
        8,
    )
    new_errors, p_hat, q_mean = call(
        functools.partial(last_kernel, devices, block),
        [vmem((1, depth, width), BF16), vmem((rank, depth)), vmem((rank, width))],
        [SM] + [VM] * 6,
        [HBM] * 3,
        [
            pltpu.VMEM((width * rank // LANES, LANES), F32),
            pltpu.VMEM((depth, width), BF16),
            pltpu.VMEM((rank, width), F32),
            pltpu.SemaphoreType.DMA((2 + steps,)),
        ],
        (ids, part, other, lower_inv, hat, hat3, merged),
        10**9,
        16,
    )
    return (new_errors, p_hat.T, q_mean.T)


def solution(mesh):
    cuts, dev = mesh.shape["cuts"], mesh.shape["dev"]
    cores = 2
    every = ("cuts", "group", "chip", "core")

    def program(inputs, cotangent, errors, previous_q):
        columns = inputs.shape[1] // (cores * LANES)
        chips = next(n for n in range(dev // cores, 0, -1) if dev // cores % n == 0 and columns % n == 0)
        groups = dev // (cores * chips)
        fine = Mesh(mesh.devices.reshape(cuts, groups, chips, cores), every)
        run = jax.shard_map(
            functools.partial(body, (cores, chips, groups, cuts)),
            mesh=fine,
            in_specs=(P(every, None), P(every, None), P(every, None, None), P()),
            out_specs=(P(every, None, None), P(), P()),
            check_vma=False,
        )
        return run(inputs, cotangent, errors, previous_q)

    return program
```

time: 239 us -> 65.6 us (0.27)
  waiting for transfers between devices: 107 us -> 23.1 us
  blocking collectives: 62.3 us -> 0 us
  matrix products: 34.7 us -> 0 us
  starting transfers between devices: 0.12 us -> 21.5 us
  Pallas kernels: 0 us -> 18 us
  between operations: 13.8 us -> 0.81 us
  other arithmetic: 12.1 us -> 0.08 us
  local copies, waits for them, and re-layouts: 8.29 us -> 1.95 us
    reduce_scatter x2 -> x0, waiting for transfers between devices: 70.4 us -> none  [the longest x1 37.8 us: body(): lax.psum_scatter(jnp.dot(merged, previous_q, precision=HI), 'dev', scatte...]
    psum x2 -> x0, blocking collectives: 42 us -> none  [the longest x1 22.4 us: body(): gram = lax.psum(contract_rows(p_share, p_share), 'dev')]
    psum x1 -> x0, waiting for transfers between devices: 36.7 us -> none  [body(): p_share = lax.psum(p_share, 'cuts')]
    dot_general x5 -> x0, matrix products: 33.6 us -> none  [the longest x2 13.9 us: contract_rows(): lax.dot_general(left, right, (((0,), (0,)), ((), ())), precision=HI, pref...]
    ppermute x0 -> x22, waiting for transfers between devices: none -> 23.1 us  [swap(): return lax.ppermute(x, axis, [(i, i ^ by) for i in range(size)])]
    ppermute x0 -> x22, starting transfers between devices: none -> 21.5 us  [swap(): return lax.ppermute(x, axis, [(i, i ^ by) for i in range(size)])]
    all_gather x2 -> x0, blocking collectives: 20.3 us -> none  [the longest x1 11.1 us: body(): p_hat = lax.all_gather(hat_share, 'dev', axis=0, tiled=True)]
    pallas_call x0 -> x16, Pallas kernels: none -> 18 us  [call(): pl.pallas_call(kernel, out_shape=outs, in_specs=ins_specs, out_specs=out_...]
  transfers between devices with their start and end apart: 3 -> 22, of which waited for: 3 -> 14; matrix products, arithmetic and copies ran while one was open for 0% -> 0% of each run, Pallas kernels for 0% -> 16%
where the time goes in v1:
time: 65.6 us; the launch traced here: 65.4 us
  waiting for transfers between devices  23.1 us (35%)
  starting transfers between devices  21.5 us (33%)
  Pallas kernels  18 us (27%)
  local copies, waits for them, and re-layouts  1.95 us (3%)
  between operations  0.81 us (1%)
    ppermute x22, waiting for transfers between devices, swap(): return lax.ppermute(x, axis, [(i, i ^ by) for i in range(size)])  23.1 us
    ppermute x22, starting transfers between devices, swap(): return lax.ppermute(x, axis, [(i, i ^ by) for i in range(size)])  21.5 us
    pallas_call x16, Pallas kernels, call(): pl.pallas_call(kernel, out_shape=outs, in_specs=ins_specs, out_specs=out_...  18 us
    unnamed x4, local copies, waits for them, and re-layouts  1.95 us
  transfers between devices with their start and end apart: 22, of which 14 were waited for; matrix products, arithmetic and copies ran while one was open for 0% of the time, Pallas kernels for 16%

profile of v1, /device:TPU:0, one launch (start us, length us, event | category | flops | bytes accessed | tf_op | source)
XLA Modules:
  0.0 65.4 jit_solution(6079672917658452111)
XLA Ops:
  0.7 1.0 %copy-done = bf16[512,512]{1,0:T(8,128)(2,1)S(1)} copy-done((bf16[512,512]{1,0:T(8,128)(2,1)S(1)}, bf16[512,512]{1,0:T(8,128)(2,1)}, u32[]{:S(2)}) %copy-start) | copy-done | bytes 524312
  2.7 3.7 %shard_map.67 = (f32[768,128]{1,0:T(8,128)S(1)}, bf16[512,3072]{1,0:T(8,128)(2,1)S(1)}, bf16[512,512]{1,0:T(8,128)(2,1)S(1)}, bf16[3072,512]{1,0:T(8,128)(2,1)S(...) custom-call(s32[2]{0:T(128)S(1)} %pad_add_fusion.ids, bf16[512,3072]{1,0:T(8,128)(2,1)} %x_hbm.1, ...), custom_call_target="tpu_custom_call" | custom-call | flops 1000000000 | tf_op jit(solution)/shard_map/pallas_call | solution.py:40
  6.9 1.6 %shard_map.68.refs_0_ = f32[768,128]{1,0:T(8,128)S(1)} custom-call(s32[2]{0:T(128)S(1)} %pad_add_fusion.ids, bf16[512,3072]{1,0:T(8,128)(2,1)S(1)} %get-tuple-element.27.xv, bf16[3072,512]{1,0:T(8,128)(2,1)S(1)} %get-tuple-element.28.ev, bf16[192,512]{1,0:T(8,128)(2,1)S(1)} %get-tuple-element.29.v3, bf16[192,512]{1,0:T(8,128)(2,1)S(1)} %get-tuple-element.30.q3), custom_call_target="tpu_custom_call" | custom-call | flops 1000000000 | tf_op jit(solution)/shard_map/pallas_call | solution.py:40
  8.5 2.7 %collective-permute-start.1 = (f32[192,128]{1,0:T(8,128)S(1)}, f32[192,128]{1,0:T(8,128)S(1)}, u32[]{:S(2)}, u32[]{:S(2)}) collective-permute-start(f32[192,128]{1,0:T(8,128)S(1)} %get-tuple-element.33), channel_id=1, source_target_pairs={{0,2},{2,0},{4,6},{6,4},{1,3},{3,1},{5,7},{7,5},{8,10},{10,8},{12,... | collective-permute-start | bytes 294920 | tf_op jit(solution)/shard_map/ppermute | solution.py:291
  11.2 1.5 %collective-permute-start.2 = (f32[192,128]{1,0:T(8,128)S(1)}, f32[192,128]{1,0:T(8,128)S(1)}, u32[]{:S(2)}, u32[]{:S(2)}) collective-permute-start(f32[192,128]{1,0:T(8,128)S(1)} %get-tuple-element.34), channel_id=1, source_target_pairs={{0,4},{2,6},{4,0},{6,2},{1,5},{3,7},{5,1},{7,3},{8,12},{10,14},{12... | collective-permute-start | bytes 294920 | tf_op jit(solution)/shard_map/ppermute | solution.py:291
  12.8 1.8 %collective-permute-done.1.refs_1_ = f32[192,128]{1,0:T(8,128)S(1)} collective-permute-done((f32[192,128]{1,0:T(8,128)S(1)}, f32[192,128]{1,0:T(8,128)S(1)}, u32[]{:S(2)}, u32[]{:S(2)}) %collective-permute-start.1) | collective-permute-done | bytes 98336 | tf_op jit(solution)/shard_map/ppermute | solution.py:291
  14.5 2.6 %collective-permute-done.2.refs_2_ = f32[192,128]{1,0:T(8,128)S(1)} collective-permute-done((f32[192,128]{1,0:T(8,128)S(1)}, f32[192,128]{1,0:T(8,128)S(1)}, u32[]{:S(2)}, u32[]{:S(2)}) %collective-permute-start.2) | collective-permute-done | bytes 98336 | tf_op jit(solution)/shard_map/ppermute | solution.py:291
  17.1 1.1 %collective-permute-done.3.refs_3_ = f32[192,128]{1,0:T(8,128)S(1)} collective-permute-done((f32[192,128]{1,0:T(8,128)S(1)}, f32[192,128]{1,0:T(8,128)S(1)}, u32[]{:S(2)}, u32[]{:S(2)}) %collective-permute-start.3) | collective-permute-done | bytes 98336 | tf_op jit(solution)/shard_map/ppermute | solution.py:291
  18.3 1.6 %collective-permute-start.4 = (f32[192,128]{1,0:T(8,128)S(1)}, f32[192,128]{1,0:T(8,128)S(1)}, u32[]{:S(2)}, u32[]{:S(2)}) collective-permute-start(f32[192,128]{1,0:T(8,128)S(1)} %shard_map.70.refs_0_), channel_id=1, source_target_pairs={{0,8},{8,0},{16,24},{24,16},{1,9},{9,1},{17,25},{25,17},{2,10},{10... | collective-permute-start | bytes 294920 | tf_op jit(solution)/shard_map/ppermute | solution.py:291
  19.9 2.6 %collective-permute-start.5 = (f32[192,128]{1,0:T(8,128)S(1)}, f32[192,128]{1,0:T(8,128)S(1)}, u32[]{:S(2)}, u32[]{:S(2)}) collective-permute-start(f32[192,128]{1,0:T(8,128)S(1)} %shard_map.70.refs_0_), channel_id=1, source_target_pairs={{0,16},{8,24},{16,0},{24,8},{1,17},{9,25},{17,1},{25,9},{2,18},{10... | collective-permute-start | bytes 294920 | tf_op jit(solution)/shard_map/ppermute | solution.py:291
  22.7 1.1 %collective-permute-done.4.refs_1_ = f32[192,128]{1,0:T(8,128)S(1)} collective-permute-done((f32[192,128]{1,0:T(8,128)S(1)}, f32[192,128]{1,0:T(8,128)S(1)}, u32[]{:S(2)}, u32[]{:S(2)}) %collective-permute-start.4) | collective-permute-done | bytes 98336 | tf_op jit(solution)/shard_map/ppermute | solution.py:291
  23.8 5.3 %collective-permute-done.5.refs_2_ = f32[192,128]{1,0:T(8,128)S(1)} collective-permute-done((f32[192,128]{1,0:T(8,128)S(1)}, f32[192,128]{1,0:T(8,128)S(1)}, u32[]{:S(2)}, u32[]{:S(2)}) %collective-permute-start.5) | collective-permute-done | bytes 98336 | tf_op jit(solution)/shard_map/ppermute | solution.py:291
  29.2 1.3 %collective-permute-start.9 = (f32[192,128]{1,0:T(8,128)S(1)}, f32[192,128]{1,0:T(8,128)S(1)}, u32[]{:S(2)}, u32[]{:S(2)}) collective-permute-start(f32[192,128]{1,0:T(8,128)S(1)} %shard_map.71.refs_0_), channel_id=1, source_target_pairs={{0,4},{2,6},{4,0},{6,2},{1,5},{3,7},{5,1},{7,3},{8,12},{10,14},{12... | collective-permute-start | bytes 294920 | tf_op jit(solution)/shard_map/ppermute | solution.py:291
  30.5 2.2 %collective-permute-start.11 = (f32[192,128]{1,0:T(8,128)S(1)}, f32[192,128]{1,0:T(8,128)S(1)}, u32[]{:S(2)}, u32[]{:S(2)}) collective-permute-start(f32[192,128]{1,0:T(8,128)S(1)} %shard_map.71.refs_0_), channel_id=1, source_target_pairs={{0,6},{2,4},{4,2},{6,0},{1,7},{3,5},{5,3},{7,1},{8,14},{10,12},{12... | collective-permute-start | bytes 294920 | tf_op jit(solution)/shard_map/ppermute | solution.py:291
  32.7 1.1 %collective-permute-done.9.refs_1_ = f32[192,128]{1,0:T(8,128)S(1)} collective-permute-done((f32[192,128]{1,0:T(8,128)S(1)}, f32[192,128]{1,0:T(8,128)S(1)}, u32[]{:S(2)}, u32[]{:S(2)}) %collective-permute-start.9) | collective-permute-done | bytes 98336 | tf_op jit(solution)/shard_map/ppermute | solution.py:291
  33.9 2.1 %collective-permute-done.11.refs_2_ = f32[192,128]{1,0:T(8,128)S(1)} collective-permute-done((f32[192,128]{1,0:T(8,128)S(1)}, f32[192,128]{1,0:T(8,128)S(1)}, u32[]{:S(2)}, u32[]{:S(2)}) %collective-permute-start.11) | collective-permute-done | bytes 98336 | tf_op jit(solution)/shard_map/ppermute | solution.py:291
  36.0 1.3 %collective-permute-done.7.refs_0_ = f32[192,128]{1,0:T(8,128)S(1)} collective-permute-done((f32[192,128]{1,0:T(8,128)S(1)}, f32[192,128]{1,0:T(8,128)S(1)}, u32[]{:S(2)}, u32[]{:S(2)}) %collective-permute-start.7) | collective-permute-done | bytes 98336 | tf_op jit(solution)/shard_map/ppermute | solution.py:291
  37.3 2.2 %shard_map.72 = (f32[3072,512]{1,0:T(8,128)S(1)}, bf16[6144,512]{1,0:T(8,128)(2,1)S(1)}) custom-call(bf16[512,3072]{1,0:T(8,128)(2,1)S(1)} %get-tuple-element.27.xv, bf16[512,512]{1,0:T(8,128)(2,1)S(1)} %get-tuple-element.36.yv, bf16[3072,512]{1,0:T(8,128)(2,1)S(1)} %get-tuple-element.28.ev), custom_call_target="tpu_custom_call" | custom-call | flops 1000000000 | tf_op jit(solution)/shard_map/pallas_call | solution.py:40
  39.5 1.0 %shard_map.73 = (bf16[192,768]{1,0:T(8,128)(2,1)S(1)}, f32[192,512]{1,0:T(8,128)S(1)}) custom-call(s32[2]{0:T(128)S(1)} %pad_add_fusion.ids, f32[192,128]{1,0:T(8,128)S(1)} %shard_map.71.refs_0_, f32[192,128]{1,0:T(8,128)S(1)} %collective-permute-done.13.refs_1_, bf16[6144,512]{1,0:T(8,128)(2,1)S(1)} %get-tuple-element.37.refs_2_.refs_3_), custom_call_target="tpu_custom_call" | custom-call | flops 100000000 | tf_op jit(solution)/shard_map/pallas_call | solution.py:40
  40.5 1.2 %shard_map.74 = (bf16[192,1152]{1,0:T(8,128)(2,1)S(1)}, f32[192,512]{1,0:T(8,128)S(1)}) custom-call(s32[2]{0:T(128)S(1)} %pad_add_fusion.ids, f32[192,128]{1,0:T(8,128)S(1)} %collective-permute-done.7.refs_0_, f32[192,128]{1,0:T(8,128)S(1)} %collective-permute-done.9.refs_1_, f32[192,128]{1,0:T(8,128)S(1)} %collective-permute-done.11.refs_2_, ...), custom_call_target="tpu_custom_call" | custom-call | flops 100000000 | tf_op jit(solution)/shard_map/pallas_call | solution.py:40
  41.8 1.2 %shard_map.75 = (bf16[192,1152]{1,0:T(8,128)(2,1)S(1)}, f32[128,128]{1,0:T(8,128)S(1)}, f32[128,128]{1,0:T(8,128)S(1)}) custom-call(s32[2]{0:T(128)S(1)} %pad_add_fusion.ids, f32[192,128]{1,0:T(8,128)S(1)} %collective-permute-done.8.refs_0_, f32[192,128]{1,0:T(8,128)S(1)} %collective-permute-done.10.refs_1_, f32[192,128]{1,0:T(8,128)S(1)} %collective-permute-done.12.refs_2_, ...), custom_call_target="tpu_custom_call" | custom-call | flops 100000000 | tf_op jit(solution)/shard_map/pallas_call | solution.py:40
  44.5 1.1 %collective-permute-start.15 = (f32[128,128]{1,0:T(8,128)S(1)}, f32[128,128]{1,0:T(8,128)S(1)}, u32[]{:S(2)}, u32[]{:S(2)}) collective-permute-start(f32[128,128]{1,0:T(8,128)S(1)} %shard_map.76.refs_0_), channel_id=1, source_target_pairs={{0,2},{2,0},{4,6},{6,4},{1,3},{3,1},{5,7},{7,5},{8,10},{10,8},{12,... | collective-permute-start | bytes 196616 | tf_op jit(solution)/shard_map/ppermute | solution.py:291
  46.4 1.7 %collective-permute-start.17 = (f32[128,128]{1,0:T(8,128)S(1)}, f32[128,128]{1,0:T(8,128)S(1)}, u32[]{:S(2)}, u32[]{:S(2)}) collective-permute-start(f32[128,128]{1,0:T(8,128)S(1)} %shard_map.76.refs_0_), channel_id=1, source_target_pairs={{0,6},{2,4},{4,2},{6,0},{1,7},{3,5},{5,3},{7,1},{8,14},{10,12},{12... | collective-permute-start | bytes 196616 | tf_op jit(solution)/shard_map/ppermute | solution.py:291
  48.9 1.7 %collective-permute-done.16.refs_2_ = f32[128,128]{1,0:T(8,128)S(1)} collective-permute-done((f32[128,128]{1,0:T(8,128)S(1)}, f32[128,128]{1,0:T(8,128)S(1)}, u32[]{:S(2)}, u32[]{:S(2)}) %collective-permute-start.16) | collective-permute-done | bytes 65568 | tf_op jit(solution)/shard_map/ppermute | solution.py:291
  51.5 1.7 %collective-permute-start.18 = (f32[128,128]{1,0:T(8,128)S(1)}, f32[128,128]{1,0:T(8,128)S(1)}, u32[]{:S(2)}, u32[]{:S(2)}) collective-permute-start(f32[128,128]{1,0:T(8,128)S(1)} %shard_map.77.refs_0_), channel_id=1, source_target_pairs={{0,8},{8,0},{16,24},{24,16},{1,9},{9,1},{17,25},{25,17},{2,10},{10... | collective-permute-start | bytes 196616 | tf_op jit(solution)/shard_map/ppermute | solution.py:291
  53.2 1.4 %collective-permute-start.19 = (f32[128,128]{1,0:T(8,128)S(1)}, f32[128,128]{1,0:T(8,128)S(1)}, u32[]{:S(2)}, u32[]{:S(2)}) collective-permute-start(f32[128,128]{1,0:T(8,128)S(1)} %shard_map.77.refs_0_), channel_id=1, source_target_pairs={{0,16},{8,24},{16,0},{24,8},{1,17},{9,25},{17,1},{25,9},{2,18},{10... | collective-permute-start | bytes 196616 | tf_op jit(solution)/shard_map/ppermute | solution.py:291
  54.7 1.3 %collective-permute-start.20 = (f32[128,128]{1,0:T(8,128)S(1)}, f32[128,128]{1,0:T(8,128)S(1)}, u32[]{:S(2)}, u32[]{:S(2)}) collective-permute-start(f32[128,128]{1,0:T(8,128)S(1)} %shard_map.77.refs_0_), channel_id=1, source_target_pairs={{0,24},{8,16},{16,8},{24,0},{1,25},{9,17},{17,9},{25,1},{2,26},{10... | collective-permute-start | bytes 196616 | tf_op jit(solution)/shard_map/ppermute | solution.py:291
  56.0 2.0 %shard_map.80.refs_3_.lower_inv = f32[64,64]{1,0:T(8,128)S(1)} custom-call(f32[64,64]{1,0:T(8,128)S(1)} %shard_map.79.gram), custom_call_target="tpu_custom_call" | custom-call | flops 1000000000 | tf_op jit(solution)/shard_map/pallas_call | solution.py:40
  58.0 1.4 %collective-permute-done.19.refs_2_ = f32[128,128]{1,0:T(8,128)S(1)} collective-permute-done((f32[128,128]{1,0:T(8,128)S(1)}, f32[128,128]{1,0:T(8,128)S(1)}, u32[]{:S(2)}, u32[]{:S(2)}) %collective-permute-start.19) | collective-permute-done | bytes 65568 | tf_op jit(solution)/shard_map/ppermute | solution.py:291
  59.4 1.4 %collective-permute-done.20.refs_3_ = f32[128,128]{1,0:T(8,128)S(1)} collective-permute-done((f32[128,128]{1,0:T(8,128)S(1)}, f32[128,128]{1,0:T(8,128)S(1)}, u32[]{:S(2)}, u32[]{:S(2)}) %collective-permute-start.20) | collective-permute-done | bytes 65568 | tf_op jit(solution)/shard_map/ppermute | solution.py:291
  60.9 1.7 %shard_map.81 = (f32[64,3072]{1,0:T(8,128)S(1)}, bf16[3072,192]{1,0:T(8,128)(2,1)S(1)}) custom-call(s32[2]{0:T(128)S(1)} %pad_add_fusion.ids, bf16[192,768]{1,0:T(8,128)(2,1)S(1)} %get-tuple-element.42.refs_0_, bf16[192,1152]{1,0:T(8,128)(2,1)S(1)} %get-tuple-element.43.refs_1_, bf16[192,1152]{1,0:T(8,128)(2,1)S(1)} %get-tuple-element.44.refs_2_, ...), custom_call_target="tpu_custom_call" | custom-call | flops 1000000000 | tf_op jit(solution)/shard_map/pallas_call | solution.py:40
  62.6 2.8 %shard_map.82 = (bf16[1,3072,512]{2,1,0:T(8,128)(2,1)}, f32[64,3072]{1,0:T(8,128)}, f32[64,512]{1,0:T(8,128)}) custom-call(s32[2]{0:T(128)S(1)} %pad_add_fusion.ids, f32[128,128]{1,0:T(8,128)S(1)} %shard_map.78.keep, f32[128,128]{1,0:T(8,128)S(1)} %collective-permute-done.21.other, f32[64,64]{1,0:T(8,128)S(1)} %shard_map.80.refs_3_.lower_inv, ...), custom_call_target="tpu_custom_call" | custom-call | flops 1000000000 | tf_op jit(solution)/shard_map/pallas_call | solution.py:40
  (33 shorter events, 6.1 us)
Async XLA Ops:
  0.7 1.0 %copy-start = (bf16[512,512]{1,0:T(8,128)(2,1)S(1)}, bf16[512,512]{1,0:T(8,128)(2,1)}, u32[]{:S(2)}) copy-start(bf16[512,512]{1,0:T(8,128)(2,1)} %y_hbm.1) | copy-start | bytes 1572868
  1.8 0.9 %copy-start.1 = (f32[512,64]{0,1:T(8,128)S(1)}, f32[512,64]{0,1:T(8,128)}, u32[]{:S(2)}) copy-start(f32[512,64]{0,1:T(8,128)} %param.7) | copy-start | bytes 393220
  6.3 2.1 %collective-permute-start = (f32[768,128]{1,0:T(8,128)S(1)}, f32[768,128]{1,0:T(8,128)S(1)}, u32[]{:S(2)}, u32[]{:S(2)}) collective-permute-start(f32[768,128]{1,0:T(8,128)S(1)} %get-tuple-element.31), channel_id=1, source_target_pairs={{0,1},{1,0},{2,3},{3,2},{4,5},{5,4},{6,7},{7,6},{8,9},{9,8},{10,11... | collective-permute-start | bytes 1179656 | tf_op jit(solution)/shard_map/ppermute | solution.py:291
  8.5 6.0 %collective-permute-start.1 = (f32[192,128]{1,0:T(8,128)S(1)}, f32[192,128]{1,0:T(8,128)S(1)}, u32[]{:S(2)}, u32[]{:S(2)}) collective-permute-start(f32[192,128]{1,0:T(8,128)S(1)} %get-tuple-element.33), channel_id=1, source_target_pairs={{0,2},{2,0},{4,6},{6,4},{1,3},{3,1},{5,7},{7,5},{8,10},{10,8},{12,... | collective-permute-start | bytes 294920 | tf_op jit(solution)/shard_map/ppermute | solution.py:291
  11.2 5.9 %collective-permute-start.2 = (f32[192,128]{1,0:T(8,128)S(1)}, f32[192,128]{1,0:T(8,128)S(1)}, u32[]{:S(2)}, u32[]{:S(2)}) collective-permute-start(f32[192,128]{1,0:T(8,128)S(1)} %get-tuple-element.34), channel_id=1, source_target_pairs={{0,4},{2,6},{4,0},{6,2},{1,5},{3,7},{5,1},{7,3},{8,12},{10,14},{12... | collective-permute-start | bytes 294920 | tf_op jit(solution)/shard_map/ppermute | solution.py:291
  12.7 5.5 %collective-permute-start.3 = (f32[192,128]{1,0:T(8,128)S(1)}, f32[192,128]{1,0:T(8,128)S(1)}, u32[]{:S(2)}, u32[]{:S(2)}) collective-permute-start(f32[192,128]{1,0:T(8,128)S(1)} %get-tuple-element.35), channel_id=1, source_target_pairs={{0,6},{2,4},{4,2},{6,0},{1,7},{3,5},{5,3},{7,1},{8,14},{10,12},{12... | collective-permute-start | bytes 294920 | tf_op jit(solution)/shard_map/ppermute | solution.py:291
  18.3 5.6 %collective-permute-start.4 = (f32[192,128]{1,0:T(8,128)S(1)}, f32[192,128]{1,0:T(8,128)S(1)}, u32[]{:S(2)}, u32[]{:S(2)}) collective-permute-start(f32[192,128]{1,0:T(8,128)S(1)} %shard_map.70.refs_0_), channel_id=1, source_target_pairs={{0,8},{8,0},{16,24},{24,16},{1,9},{9,1},{17,25},{25,17},{2,10},{10... | collective-permute-start | bytes 294920 | tf_op jit(solution)/shard_map/ppermute | solution.py:291
  19.9 9.2 %collective-permute-start.5 = (f32[192,128]{1,0:T(8,128)S(1)}, f32[192,128]{1,0:T(8,128)S(1)}, u32[]{:S(2)}, u32[]{:S(2)}) collective-permute-start(f32[192,128]{1,0:T(8,128)S(1)} %shard_map.70.refs_0_), channel_id=1, source_target_pairs={{0,16},{8,24},{16,0},{24,8},{1,17},{9,25},{17,1},{25,9},{2,18},{10... | collective-permute-start | bytes 294920 | tf_op jit(solution)/shard_map/ppermute | solution.py:291
  22.5 6.7 %collective-permute-start.6 = (f32[192,128]{1,0:T(8,128)S(1)}, f32[192,128]{1,0:T(8,128)S(1)}, u32[]{:S(2)}, u32[]{:S(2)}) collective-permute-start(f32[192,128]{1,0:T(8,128)S(1)} %shard_map.70.refs_0_), channel_id=1, source_target_pairs={{0,24},{8,16},{16,8},{24,0},{1,25},{9,17},{17,9},{25,1},{2,26},{10... | collective-permute-start | bytes 294920 | tf_op jit(solution)/shard_map/ppermute | solution.py:291
  29.2 4.7 %collective-permute-start.9 = (f32[192,128]{1,0:T(8,128)S(1)}, f32[192,128]{1,0:T(8,128)S(1)}, u32[]{:S(2)}, u32[]{:S(2)}) collective-permute-start(f32[192,128]{1,0:T(8,128)S(1)} %shard_map.71.refs_0_), channel_id=1, source_target_pairs={{0,4},{2,6},{4,0},{6,2},{1,5},{3,7},{5,1},{7,3},{8,12},{10,14},{12... | collective-permute-start | bytes 294920 | tf_op jit(solution)/shard_map/ppermute | solution.py:291
  30.5 5.5 %collective-permute-start.11 = (f32[192,128]{1,0:T(8,128)S(1)}, f32[192,128]{1,0:T(8,128)S(1)}, u32[]{:S(2)}, u32[]{:S(2)}) collective-permute-start(f32[192,128]{1,0:T(8,128)S(1)} %shard_map.71.refs_0_), channel_id=1, source_target_pairs={{0,6},{2,4},{4,2},{6,0},{1,7},{3,5},{5,3},{7,1},{8,14},{10,12},{12... | collective-permute-start | bytes 294920 | tf_op jit(solution)/shard_map/ppermute | solution.py:291
  32.7 4.6 %collective-permute-start.7 = (f32[192,128]{1,0:T(8,128)S(1)}, f32[192,128]{1,0:T(8,128)S(1)}, u32[]{:S(2)}, u32[]{:S(2)}) collective-permute-start(f32[192,128]{1,0:T(8,128)S(1)} %shard_map.71.refs_0_), channel_id=1, source_target_pairs={{0,2},{2,0},{4,6},{6,4},{1,3},{3,1},{5,7},{7,5},{8,10},{10,8},{12,... | collective-permute-start | bytes 294920 | tf_op jit(solution)/shard_map/ppermute | solution.py:291
  32.7 6.8 %collective-permute-start.13 = (f32[192,128]{1,0:T(8,128)S(1)}, f32[192,128]{1,0:T(8,128)S(1)}, u32[]{:S(2)}, u32[]{:S(2)}) collective-permute-start(f32[192,128]{1,0:T(8,128)S(1)} %shard_map.71.refs_0_), channel_id=1, source_target_pairs={{0,1},{1,0},{2,3},{3,2},{4,5},{5,4},{6,7},{7,6},{8,9},{9,8},{10,11... | collective-permute-start | bytes 294920 | tf_op jit(solution)/shard_map/ppermute | solution.py:291
  33.9 7.9 %collective-permute-start.10 = (f32[192,128]{1,0:T(8,128)S(1)}, f32[192,128]{1,0:T(8,128)S(1)}, u32[]{:S(2)}, u32[]{:S(2)}) collective-permute-start(f32[192,128]{1,0:T(8,128)S(1)} %collective-permute-done.9.refs_1_), channel_id=1, source_target_pairs={{0,1},{1,0},{2,3},{3,2},{4,5},{5,4},{6,7},{7,6},{8,9},{9,8},{10,11... | collective-permute-start | bytes 294920 | tf_op jit(solution)/shard_map/ppermute | solution.py:291
  36.0 5.7 %collective-permute-start.12 = (f32[192,128]{1,0:T(8,128)S(1)}, f32[192,128]{1,0:T(8,128)S(1)}, u32[]{:S(2)}, u32[]{:S(2)}) collective-permute-start(f32[192,128]{1,0:T(8,128)S(1)} %collective-permute-done.11.refs_2_), channel_id=1, source_target_pairs={{0,1},{1,0},{2,3},{3,2},{4,5},{5,4},{6,7},{7,6},{8,9},{9,8},{10,11... | collective-permute-start | bytes 294920 | tf_op jit(solution)/shard_map/ppermute | solution.py:291
  37.3 4.5 %collective-permute-start.8 = (f32[192,128]{1,0:T(8,128)S(1)}, f32[192,128]{1,0:T(8,128)S(1)}, u32[]{:S(2)}, u32[]{:S(2)}) collective-permute-start(f32[192,128]{1,0:T(8,128)S(1)} %collective-permute-done.7.refs_0_), channel_id=1, source_target_pairs={{0,1},{1,0},{2,3},{3,2},{4,5},{5,4},{6,7},{7,6},{8,9},{9,8},{10,11... | collective-permute-start | bytes 294920 | tf_op jit(solution)/shard_map/ppermute | solution.py:291
  43.0 1.5 %collective-permute-start.14 = (f32[128,128]{1,0:T(8,128)S(1)}, f32[128,128]{1,0:T(8,128)S(1)}, u32[]{:S(2)}, u32[]{:S(2)}) collective-permute-start(f32[128,128]{1,0:T(8,128)S(1)} %get-tuple-element.41), channel_id=1, source_target_pairs={{0,1},{1,0},{2,3},{3,2},{4,5},{5,4},{6,7},{7,6},{8,9},{9,8},{10,11... | collective-permute-start | bytes 196616 | tf_op jit(solution)/shard_map/ppermute | solution.py:291
  44.5 4.4 %collective-permute-start.15 = (f32[128,128]{1,0:T(8,128)S(1)}, f32[128,128]{1,0:T(8,128)S(1)}, u32[]{:S(2)}, u32[]{:S(2)}) collective-permute-start(f32[128,128]{1,0:T(8,128)S(1)} %shard_map.76.refs_0_), channel_id=1, source_target_pairs={{0,2},{2,0},{4,6},{6,4},{1,3},{3,1},{5,7},{7,5},{8,10},{10,8},{12,... | collective-permute-start | bytes 196616 | tf_op jit(solution)/shard_map/ppermute | solution.py:291
  45.6 5.0 %collective-permute-start.16 = (f32[128,128]{1,0:T(8,128)S(1)}, f32[128,128]{1,0:T(8,128)S(1)}, u32[]{:S(2)}, u32[]{:S(2)}) collective-permute-start(f32[128,128]{1,0:T(8,128)S(1)} %shard_map.76.refs_0_), channel_id=1, source_target_pairs={{0,4},{2,6},{4,0},{6,2},{1,5},{3,7},{5,1},{7,3},{8,12},{10,14},{12... | collective-permute-start | bytes 196616 | tf_op jit(solution)/shard_map/ppermute | solution.py:291
  46.4 5.2 %collective-permute-start.17 = (f32[128,128]{1,0:T(8,128)S(1)}, f32[128,128]{1,0:T(8,128)S(1)}, u32[]{:S(2)}, u32[]{:S(2)}) collective-permute-start(f32[128,128]{1,0:T(8,128)S(1)} %shard_map.76.refs_0_), channel_id=1, source_target_pairs={{0,6},{2,4},{4,2},{6,0},{1,7},{3,5},{5,3},{7,1},{8,14},{10,12},{12... | collective-permute-start | bytes 196616 | tf_op jit(solution)/shard_map/ppermute | solution.py:291
  51.5 6.4 %collective-permute-start.18 = (f32[128,128]{1,0:T(8,128)S(1)}, f32[128,128]{1,0:T(8,128)S(1)}, u32[]{:S(2)}, u32[]{:S(2)}) collective-permute-start(f32[128,128]{1,0:T(8,128)S(1)} %shard_map.77.refs_0_), channel_id=1, source_target_pairs={{0,8},{8,0},{16,24},{24,16},{1,9},{9,1},{17,25},{25,17},{2,10},{10... | collective-permute-start | bytes 196616 | tf_op jit(solution)/shard_map/ppermute | solution.py:291
  53.2 6.1 %collective-permute-start.19 = (f32[128,128]{1,0:T(8,128)S(1)}, f32[128,128]{1,0:T(8,128)S(1)}, u32[]{:S(2)}, u32[]{:S(2)}) collective-permute-start(f32[128,128]{1,0:T(8,128)S(1)} %shard_map.77.refs_0_), channel_id=1, source_target_pairs={{0,16},{8,24},{16,0},{24,8},{1,17},{9,25},{17,1},{25,9},{2,18},{10... | collective-permute-start | bytes 196616 | tf_op jit(solution)/shard_map/ppermute | solution.py:291
  54.7 6.1 %collective-permute-start.20 = (f32[128,128]{1,0:T(8,128)S(1)}, f32[128,128]{1,0:T(8,128)S(1)}, u32[]{:S(2)}, u32[]{:S(2)}) collective-permute-start(f32[128,128]{1,0:T(8,128)S(1)} %shard_map.77.refs_0_), channel_id=1, source_target_pairs={{0,24},{8,16},{16,8},{24,0},{1,25},{9,17},{17,9},{25,1},{2,26},{10... | collective-permute-start | bytes 196616 | tf_op jit(solution)/shard_map/ppermute | solution.py:291
  60.8 1.8 %collective-permute-start.21 = (f32[128,128]{1,0:T(8,128)S(1)}, f32[128,128]{1,0:T(8,128)S(1)}, u32[]{:S(2)}, u32[]{:S(2)}) collective-permute-start(f32[128,128]{1,0:T(8,128)S(1)} %shard_map.78.keep), channel_id=1, source_target_pairs={{0,1},{1,0},{2,3},{3,2},{4,5},{5,4},{6,7},{7,6},{8,9},{9,8},{10,11... | collective-permute-start | bytes 196616 | tf_op jit(solution)/shard_map/ppermute | solution.py:291
